TPU v7x, 256 devices: a whole 4x4x8 slice. The times are simulated.
256 devices in a mesh: expert: 16 (over y, x), dp: 16 (over z, core).
Axes of the slice: x: 4, y: 4, z: 8, core: 2. Of those that a mesh axis runs over, the one named last changes fastest.
Arguments:
- acts: bfloat16 [256, 16, 16, 3584], P(('expert', 'dp')), may hold values from -6 to 6
- grad_out: bfloat16 [256, 16, 16, 1024], P(('expert', 'dp')), may hold values from -0.125 to 0.125
- routing_counts: int32 [256, 16], P(('expert', 'dp')), may hold values from 1 to 16, as said below
- left_basis: bfloat16 [16, 3584, 3584], P('expert', 'dp'), may hold values from -1 to 1, as said below
- right_basis: bfloat16 [16, 1024, 1024], P('expert'), may hold values from -1 to 1, as said below
- first_moment: float32 [16, 3584, 1024], P('expert', 'dp'), may hold values from -3 to 3
- second_moment: float32 [16, 3584, 1024], P('expert', 'dp'), may hold values from 0.05 to 2000
Outputs:
- step_delta: bfloat16 [16, 3584, 1024], P('expert', 'dp')
- first_out: float32 [16, 3584, 1024], P('expert', 'dp')
- second_out: float32 [16, 3584, 1024], P('expert', 'dp')
- expert_rms: float32 [16], P('expert')
Inputs may be any that keep to these rules, and one draw needn't show every extreme that they name: Slot s of shard i for expert e carries a routed token when s < routing_counts[i, e]; the other slots hold leftover values that belong to no token. In every shard some expert has all 16 slots live. `left_basis`: each expert's block is an orthogonal matrix rounded to bfloat16. `right_basis`: each expert's block is an orthogonal matrix rounded to bfloat16.
All inputs are finite; a program needn't handle non-finite values.
Results may differ from a plain program's by a relative error of at most 0.013.
Values may be sent and summed in bfloat16 or wider, within the bound.
A program may use at most 64 MiB of HBM per device.

v0:
```python
import functools

import jax
import jax.numpy as jnp
from jax import lax
from jax.sharding import Mesh
from jax.sharding import PartitionSpec as P

EXPERT = ("expert_0", "expert_1")
DP = ("dp_0", "dp_1")
EXPERT_DP = ("expert_0", "expert_1", "dp_0", "dp_1")


BETA_ONE = 0.9
BETA_TWO = 0.95
EPS_DIVIDE = 1e-08
EPS_MEAN = 1e-06


def sent_together(arrays, axis, split_dim, concat_dim, along):
    both = jnp.concatenate(arrays, axis=along)
    filled, at, gathered = (
        lax.all_to_all(both, axis, split_axis=split_dim, concat_axis=concat_dim, tiled=True),
        0,
        [],
    )
    for a in arrays:
        gathered.append(lax.slice_in_dim(filled, at, at + a.shape[along], axis=along))
        at += a.shape[along]
    return tuple(gathered)


def over_axes(x, axes):
    return functools.reduce(lax.psum, axes, x)


def local(acts, grad_out, routing_counts, left_basis, right_basis, first_moment, second_moment):
    slot_count = acts.shape[2]
    slot_index = lax.broadcasted_iota(jnp.int32, routing_counts.shape + (slot_count,), 2)
    live_slots = (slot_index < routing_counts[:, :, None])[..., None]
    acts_live = jnp.where(live_slots, acts, jnp.zeros((), jnp.bfloat16))
    grads_live = jnp.where(live_slots, grad_out, jnp.zeros((), jnp.bfloat16))
    came_acts, came_grads = sent_together((acts_live, grads_live), EXPERT, 1, 0, 3)
    model_width = came_acts.shape[-1]
    hidden_width = came_grads.shape[-1]
    token_acts = came_acts.reshape(-1, model_width)
    token_grads = came_grads.reshape(-1, hidden_width)
    summed = lax.psum_scatter(
        jnp.einsum("tk,tf->kf", token_acts, token_grads, preferred_element_type=jnp.float32).astype(
            jnp.bfloat16
        ),
        DP,
        scatter_dimension=0,
        tiled=True,
    )
    right_block = right_basis[0]
    left_rows = left_basis[0]
    right_turned = jnp.dot(summed, right_block, preferred_element_type=jnp.float32).astype(
        jnp.bfloat16
    )
    basis_columns = left_rows
    rotated = lax.psum_scatter(
        jnp.einsum(
            "kc,kf->cf", basis_columns, right_turned, preferred_element_type=jnp.float32
        ).astype(jnp.bfloat16),
        DP,
        scatter_dimension=0,
        tiled=True,
    ).astype(jnp.float32)
    first_new = BETA_ONE * first_moment[0] + (1.0 - BETA_ONE) * rotated
    second_new = BETA_TWO * second_moment[0] + (1.0 - BETA_TWO) * rotated * rotated
    direction = (first_new / (jnp.sqrt(second_new) + EPS_DIVIDE)).astype(jnp.bfloat16)
    restored = jnp.einsum(
        "kg,fg->kf", direction, right_block, preferred_element_type=jnp.float32
    ).astype(jnp.bfloat16)
    basis_columns = left_rows
    update = jnp.dot(
        basis_columns,
        lax.all_gather(restored, DP, axis=0, tiled=True),
        preferred_element_type=jnp.float32,
    )
    squares = jnp.sum(update * update)
    cell_total = float(model_width * hidden_width)
    expert_slots = lax.broadcasted_iota(jnp.int32, (lax.axis_size(EXPERT),), 0)
    mine = expert_slots == lax.axis_index(EXPERT)
    spread = jnp.where(mine, squares, jnp.zeros((), jnp.float32))
    all_squares = over_axes(spread, EXPERT_DP)
    all_norms = jnp.sqrt(all_squares / cell_total + EPS_MEAN)
    mean_norm = jnp.mean(all_norms)
    own_norm = jnp.sum(jnp.where(mine, all_norms, jnp.zeros((), jnp.float32)))
    step_delta = (-update / jnp.maximum(own_norm, mean_norm)).astype(jnp.bfloat16)
    return (step_delta[None], first_new[None], second_new[None], own_norm.reshape(1))


def solution(mesh):
    split = Mesh(mesh.devices.reshape(4, 4, 8, 2), ("expert_0", "expert_1", "dp_0", "dp_1"))
    placed = (
        P(EXPERT_DP, None, None, None),
        P(EXPERT_DP, None, None, None),
        P(EXPERT_DP, None),
        P(EXPERT, DP, None),
        P(EXPERT, None, None),
        P(EXPERT, DP, None),
        P(EXPERT, DP, None),
    )
    return jax.shard_map(
        local,
        mesh=split,
        in_specs=placed,
        out_specs=(P(EXPERT, DP, None), P(EXPERT, DP, None), P(EXPERT, DP, None), P(EXPERT)),
        check_vma=False,
    )
```

profile of v0, /device:TPU:1, one launch (start us, length us, event | category | flops | bytes accessed | tf_op | source)
XLA Modules:
  0.0 317.9 jit_solution(18019580845067574822)
XLA Ops:
  7.2 0.0 reduce-scatter.5.cloned.1.call-start
  7.2 0.9 iota_compare_fusion
  8.1 1.7 bitcast_select_fusion
  9.8 0.1 bitcast_select_fusion.1
  10.0 0.2 pad_maximum_fusion
  10.1 37.8 %all_to_all.12 = bf16[1,16,16,4608]{3,2,0,1:T(8,128)(2,1)S(1)} all-to-all(bf16[1,16,16,4608]{3,2,0,1:T(8,128)(2,1)S(1)} %pad_maximum_fusion), channel_id=1, replica_groups=mesh['expert_0'=4,'expert_1'=4,'dp_0'=8,'dp_1'=2] {'expert_0','expert_1'}, dimensions={1} | all-to-all | bytes 4718592 | tf_op jit(solution)/shard_map/all_to_all | solution.py:23
  47.9 5.1 %bitcast_convert_fusion = bf16[3584,1024]{1,0:T(8,128)(2,1)} fusion(bf16[16,1,16,4608]{3,2,0,1:T(8,128)(2,1)S(1)} %bitcast.60), kind=kOutput, calls=%fused_computation | convolution fusion | flops 1882718208 | bytes 9699328 | tf_op jit(solution)/shard_map/tk,tf->kf/dot_general | solution.py:49
  53.0 0.0 reduce-scatter.5.cloned.1.call-update
  53.0 0.0 reduce-scatter.7.cloned.1.call-start
  53.0 66.2 %reduce-scatter.5.cloned.1.call-done = bf16[224,1024]{1,0:T(8,128)(2,1)} async-done(((bf16[3584,1024]{1,0:T(8,128)(2,1)}), bf16[224,1024]{1,0:T(8,128)(2,1)}) %reduce-scatter.5.cloned.1.call-update) | async-done | bytes 458768 | tf_op jit(solution)/shard_map/reduce_scatter | solution.py:48
  119.2 7.2 %fusion = bf16[3584,1024]{0,1:T(8,128)(2,1)} fusion(bf16[1,224,3584]{2,1,0:T(8,128)(2,1)} %param.10, bf16[224,1024]{1,0:T(8,128)(2,1)} %reduce-scatter.5.cloned.1.call-done, bf16[1,1024,1024]{2,1,0:T(8,128)(2,1)S(1)} %copy-done), kind=kOutput, calls=%fused_computation.2 | convolution fusion | flops 2117828608 | bytes 11501568 | tf_op jit(solution)/shard_map/kc,kf->cf/dot_general | solution.py:63
  126.4 10.4 %copy.21 = bf16[3584,1024]{1,0:T(8,128)(2,1)} copy(bf16[3584,1024]{0,1:T(8,128)(2,1)} %fusion) | data formatting | bytes 14680064
  136.8 0.0 reduce-scatter.7.cloned.1.call-update
  136.8 0.0 all-gather.2.cloned.1.call-start
  136.9 1.5 copy.15
  138.4 2.5 copy.18
  140.9 63.6 %reduce-scatter.7.cloned.1.call-done = bf16[224,1024]{1,0:T(8,128)(2,1)} async-done(((bf16[3584,1024]{1,0:T(8,128)(2,1)}), bf16[224,1024]{1,0:T(8,128)(2,1)}) %reduce-scatter.7.cloned.1.call-update) | async-done | bytes 458768
  204.5 2.0 copy.22
  206.5 3.5 %fusion.11 = bf16[224,1024]{1,0:T(8,128)(2,1)} fusion(bf16[1,1024,1024]{2,1,0:T(8,128)(2,1)S(1)} %copy-done, bf16[224,1024]{0,1:T(8,128)(2,1)} %copy.22, f32[1,224,1024]{1,2,0:T(8,128)S(1)} %copy.15, f32[1,224,1024]{1,2,0:T(8,128)} %copy.18), kind=kOutput, calls=%fused_computation.16 | convolution fusion | flops 472514560 | bytes 4849664 | tf_op jit(solution)/shard_map/kg,fg->kf/dot_general | solution.py:73
  210.0 0.0 all-gather.2.cloned.1.call-update
  210.0 3.1 fusion.19
  213.1 2.6 copy.19
  215.7 1.2 copy.20
  216.9 46.2 %all-gather.2.cloned.1.call-done = bf16[3584,1024]{1,0:T(8,128)(2,1)} async-done(((bf16[224,1024]{1,0:T(8,128)(2,1)}), bf16[3584,1024]{1,0:T(8,128)(2,1)}) %all-gather.2.cloned.1.call-update) | async-done | bytes 7340048 | tf_op jit(solution)/shard_map/all_gather | solution.py:79
  263.1 6.1 %multiply_reduce_fusion = (f32[]{:T(128)}, f32[1024,224]{0,1:T(8,128)S(1)}) fusion(bf16[3584,1024]{1,0:T(8,128)(2,1)} %all-gather.2.cloned.1.call-done, bf16[1,224,3584]{2,1,0:T(8,128)(2,1)} %param.10), kind=kOutput, calls=%fused_computation.21 | convolution fusion | flops 1644625920 | bytes 9863172 | tf_op jit(solution)/shard_map/dot_general | solution.py:77
  269.2 0.6 compare_select_fusion.1
  269.8 8.5 %psum.28 = f32[16]{0:T(128)S(1)} all-reduce(f32[16]{0:T(128)S(1)} %compare_select_fusion.1), channel_id=1, replica_groups=mesh['expert_0'=4,'expert_1'=4,'dp_0'=8,'dp_1'=2] {'expert_0'}, use_global_device_ids=true, to_apply=%region_3.4 | all-reduce | flops 16 | bytes 128 | tf_op jit(solution)/shard_map/psum | solution.py:34
  278.3 8.4 %psum.29 = f32[16]{0:T(128)S(1)} all-reduce(f32[16]{0:T(128)S(1)} %psum.28), channel_id=1, replica_groups=mesh['expert_0'=4,'expert_1'=4,'dp_0'=8,'dp_1'=2] {'expert_1'}, use_global_device_ids=true, to_apply=%region_4.5 | all-reduce | flops 16 | bytes 128 | tf_op jit(solution)/shard_map/psum | solution.py:34
  286.7 11.7 %psum.30 = f32[16]{0:T(128)S(1)} all-reduce(f32[16]{0:T(128)S(1)} %psum.29), channel_id=1, replica_groups=mesh['expert_0'=4,'expert_1'=4,'dp_0'=8,'dp_1'=2] {'dp_0'}, use_global_device_ids=true, to_apply=%region_5.6 | all-reduce | flops 16 | bytes 128 | tf_op jit(solution)/shard_map/psum | solution.py:34
  298.4 10.2 %psum.31 = f32[16]{0:T(128)S(1)} all-reduce(f32[16]{0:T(128)S(1)} %psum.30), channel_id=1, replica_groups=mesh['expert_0'=4,'expert_1'=4,'dp_0'=8,'dp_1'=2] {'dp_1'}, use_global_device_ids=true, to_apply=%region_6.7 | all-reduce | flops 16 | bytes 128 | tf_op jit(solution)/shard_map/psum | solution.py:34
  308.6 0.6 fusion.32
  310.5 0.9 fusion.25
  (6 shorter events, 0.0 us)
Async XLA Ops:
  7.2 112.0 %copy-start = (bf16[1,1024,1024]{2,1,0:T(8,128)(2,1)S(1)}, bf16[1,1024,1024]{2,1,0:T(8,128)(2,1)}, u32[]{:S(2)}) copy-start(bf16[1,1024,1024]{2,1,0:T(8,128)(2,1)} %param.11) | copy-start | bytes 6291460
  7.2 2.7 copy-start.2
  7.2 112.0 %reduce-scatter.5.cloned.1.call-start = ((), (), s32[]{:S(2)}) async-start(), calls=%async_computation.3 | async-start | bytes 7798784 | tf_op jit(solution)/shard_map/reduce_scatter | solution.py:48
  53.0 151.5 %reduce-scatter.7.cloned.1.call-start = ((), (), s32[]{:S(2)}) async-start(), calls=%async_computation.5 | async-start | bytes 7798784
  136.8 126.3 %all-gather.2.cloned.1.call-start = ((), (), s32[]{:S(2)}) async-start(), calls=%async_computation.4 | async-start | bytes 7798784 | tf_op jit(solution)/shard_map/all_gather | solution.py:79
  213.1 2.6 copy-start.1
Sparse Core Ops, SparseCore 0:
  53.1 66.0 reduce-scatter.4
  137.0 67.5 reduce-scatter.6
  210.1 52.9 all-gather.1
where the time goes:
time: 319 us; the launch traced here: 318 us
  waiting for transfers between devices  176 us (55%)
  blocking collectives  76.5 us (24%)
  matrix products  21.8 us (7%)
  local copies, waits for them, and re-layouts  20.3 us (6%)
  between operations  15.1 us (5%)
  other arithmetic  8.07 us (3%)
    reduce_scatter x1, waiting for transfers between devices, local(): lax.psum_scatter(jnp.einsum('tk,tf->kf', token_acts, token_grads, preferr...  66.2 us
    unnamed x4, waiting for transfers between devices  63.7 us
    all_gather x1, waiting for transfers between devices, local(): lax.all_gather(restored, DP, axis=0, tiled=True)  46.2 us
    psum x4, blocking collectives, over_axes(): return functools.reduce(lax.psum, axes, x)  38.8 us
    all_to_all x1, blocking collectives, sent_together(): lax.all_to_all(both, axis, split_axis=split_dim, concat_axis=concat_dim,...  37.8 us
    unnamed x12, local copies, waits for them, and re-layouts  20.3 us
    dot_general x1, matrix products, local(): jnp.einsum('kc,kf->cf', basis_columns, right_turned, preferred_element_ty...  7.2 us
  transfers between devices with their start and end apart: 3, of which 3 were waited for; matrix products, arithmetic and copies ran while one was open for 3% of the time, Pallas kernels for 0%

commit v1 on v0

v1 whole, which is shorter than its diff:
```python
import functools

import jax
import jax.numpy as jnp
from jax import lax
from jax.experimental import pallas as pl
from jax.experimental.pallas import tpu as pltpu
from jax.sharding import Mesh
from jax.sharding import PartitionSpec as P

AXES = ("y", "x", "z", "core")
EXPERT = ("y", "x")
DP = ("z", "core")
NY, NX, NZ, NC = 4, 4, 8, 2
MESH = pl.DeviceIdType.MESH

BETA_ONE = 0.9
BETA_TWO = 0.95
EPS_DIVIDE = 1e-08
EPS_MEAN = 1e-06

PLANE = (
    (0, 1), (1, 0), (0, 3), (3, 0), (1, 1), (3, 3), (1, 3), (3, 1),
    (2, 0), (0, 2), (1, 2), (2, 1), (3, 2), (2, 3), (2, 2),
)
COLUMN = tuple((dz, dc) for dz in range(NZ) for dc in range(NC) if dz or dc)
REDUCE = ((4, 0), (3, 1), (3, 0), (2, 1), (2, 0), (1, 1), (1, 0))
ADDS = (None, None, 0, 1, 2, 3, 4)
GATHER = ((0, 0), (0, 1), (1, 0), (1, 1), (2, 0), (2, 1), (3, 0))


def kernel(
    counts, acts, grads, left, right, first_in, second_in,
    delta_out, first_out, second_out, rms_out,
    a_all, g_own, g_all, l_all, r_all, m1, m2, g_turned, part, s_one, v_one, s_two, v_two,
    turned, rot, rot_send, res_send, x_all, upd, upd_other, d_buf, f_buf, s_buf,
    n_col, n_exp,
    load_sem, a_send, a_recv, g_send, g_recv, fwd_send, fwd_recv, pair_send, pair_recv,
    r_send, r_recv, x_send, x_recv, n_send, n_recv, out_sem,
):
    y, x, z, c = (lax.axis_index(a) for a in AXES)
    other = 1 - c
    rows = left.shape[0]
    block = 2 * rows
    width = left.shape[1]
    hidden = grads.shape[1]
    half = hidden // 2
    quarter = half // 2
    slots = acts.shape[0] // (NY * NX)
    tokens = NY * NX * slots
    pair_wide = 2 * block

    def mod(v, n):
        return lax.rem(v + n, n)

    partner = (y, x, z, other)
    plane = [(mod(y + dy, NY), mod(x + dx, NX), z, c) for dy, dx in PLANE]
    column = [(y, x, mod(z + dz, NZ), mod(c + dc, NC)) for dz, dc in COLUMN]
    up = (y, x, mod(z + 1, NZ), c)
    down = (y, x, mod(z - 1, NZ), c)

    def remote(src, dst, send, recv, device):
        return pltpu.make_async_remote_copy(
            src_ref=src, dst_ref=dst, send_sem=send, recv_sem=recv, device_id=device, device_id_type=MESH
        )

    barrier = pltpu.get_barrier_semaphore()
    for device in plane + column:
        pl.semaphore_signal(barrier, 1, device_id=device, device_id_type=MESH)

    own_expert = y * NX + x
    mine_l = pl.ds(pl.multiple_of(c * rows, rows), rows)
    load_g = pltpu.make_async_copy(grads, g_own, load_sem.at[0])
    load_a = pltpu.make_async_copy(
        acts.at[pl.ds(pl.multiple_of(own_expert * slots, slots), slots), :],
        a_all.at[pl.ds(pl.multiple_of(c * tokens, tokens), slots), :],
        load_sem.at[1],
    )
    load_l = pltpu.make_async_copy(left, l_all.at[mine_l, :], load_sem.at[2])
    load_r = pltpu.make_async_copy(right, r_all, load_sem.at[3])
    load_m1 = pltpu.make_async_copy(first_in, m1, load_sem.at[4])
    load_m2 = pltpu.make_async_copy(second_in, m2, load_sem.at[5])
    for load in (load_g, load_a, load_l, load_r, load_m1, load_m2):
        load.start()
    load_g.wait()
    slot_index = lax.broadcasted_iota(jnp.int32, (slots, hidden), 0)
    for e in range(NY * NX):
        here = slice(e * slots, (e + 1) * slots)
        g_own[here, :] = jnp.where(slot_index < counts[0, e], g_own[here, :].astype(jnp.float32), 0.0).astype(jnp.bfloat16)
    pl.semaphore_wait(barrier, len(plane) + len(column))

    def token_rows(core, i):
        return pl.ds(pl.multiple_of(core * tokens + i * slots, slots), slots)

    g_copies, a_copies = [], []
    for i, ((dy, dx), device) in enumerate(zip(PLANE, plane)):
        expert = device[0] * NX + device[1]
        src = pl.ds(pl.multiple_of(expert * slots, slots), slots)
        dst = token_rows(c, i + 1)
        g_copies.append(remote(g_own.at[src, :], g_all.at[dst, :], g_send.at[i], g_recv.at[i], device))
        a_copies.append(remote(acts.at[src, :], a_all.at[dst, :], a_send.at[i], a_recv.at[i], device))
    for copy in g_copies:
        copy.start()
    for copy in a_copies:
        copy.start()
    own_g = pl.ds(pl.multiple_of(own_expert * slots, slots), slots)
    g_all[token_rows(c, 0), :] = g_own[own_g, :]
    load_a.wait()
    load_l.wait()
    l_copy = remote(l_all.at[mine_l, :], l_all.at[mine_l, :], pair_send.at[0], pair_recv.at[0], partner)
    l_copy.start()
    forwards = []
    for i in range(NY * NX):
        here = token_rows(c, i)
        forwards.append(remote(g_all.at[here, :], g_all.at[here, :], fwd_send.at[i], fwd_recv.at[0], partner))
        if i:
            g_copies[i - 1].wait_recv()
        forwards[-1].start()
    load_r.wait()
    load_m1.wait()
    load_m2.wait()
    for i in range(NY * NX):
        here = token_rows(c, i)
        forwards.append(remote(a_all.at[here, :], a_all.at[here, :], fwd_send.at[NY * NX + i], fwd_recv.at[1], partner))
        if i:
            a_copies[i - 1].wait_recv()
        forwards[-1].start()
    theirs = pl.ds(pl.multiple_of(other * tokens, tokens), tokens)
    remote(g_all.at[theirs, :], g_all.at[theirs, :], fwd_send.at[0], fwd_recv.at[0], partner).wait_recv()
    g_turned[...] = jnp.dot(
        g_all[...], r_all[:, pl.ds(pl.multiple_of(c * half, half), half)], preferred_element_type=jnp.float32
    ).astype(jnp.bfloat16)
    remote(a_all.at[theirs, :], a_all.at[theirs, :], fwd_send.at[0], fwd_recv.at[1], partner).wait_recv()
    l_copy.wait_recv()

    def reduce(lhs, rhs, send_buf, recv_buf, sems, finish):
        copies = []
        for k, (away, part_of) in enumerate(REDUCE):
            ways = []
            for way, device in ((0, up), (1, down)):
                ways.append(
                    remote(
                        send_buf.at[way, k], recv_buf.at[way, k],
                        r_send.at[sems, way, k], r_recv.at[sems, way, k], device,
                    )
                )
            copies.append(ways)

        def rows_of(away, way):
            owner = mod(z + away, NZ) if way == 0 else mod(z - away, NZ)
            return pl.multiple_of(owner * block, block)

        chunk = block // 4

        def send(k):
            away, part_of = REDUCE[k]
            for way in range(2):
                cols = slice((part_of ^ way) * quarter, ((part_of ^ way) + 1) * quarter)
                start = rows_of(away, way)
                if ADDS[k] is not None:
                    copies[ADDS[k]][way].wait_recv()

                def one(t, _):
                    at = pl.multiple_of(t * chunk, chunk)
                    value = part[pl.ds(start + at, chunk), cols]
                    if ADDS[k] is not None:
                        value = value + recv_buf[way, ADDS[k], pl.ds(at, chunk), :].astype(jnp.float32)
                    send_buf[way, k, pl.ds(at, chunk), :] = value.astype(jnp.bfloat16)
                    return 0

                lax.fori_loop(0, 4, one, 0)
                copies[k][way].start()

        def one_pair(i, _):
            which = lax.rem(z // 2 + 2 + i, NZ // 2)
            at = pl.multiple_of(which * pair_wide, pair_wide)
            part[pl.ds(at, pair_wide), :] = lax.dot_general(
                lhs[:, pl.ds(at, pair_wide)], rhs[...], (((0,), (0,)), ((), ())), preferred_element_type=jnp.float32
            )

            @pl.when(i == 0)
            def _():
                send(0)

            return 0

        lax.fori_loop(0, NZ // 2, one_pair, 0)
        for k in range(1, len(REDUCE)):
            send(k)
        own = pl.multiple_of(z * block, block)
        for k in (len(REDUCE) - 2, len(REDUCE) - 1):
            for way in range(2):
                copies[k][way].wait_recv()
        last, before = len(REDUCE) - 1, len(REDUCE) - 2

        def close(t, _):
            at = pl.multiple_of(t * chunk, chunk)
            for q in range(2):
                up_k, down_k = (last, before) if q == 0 else (before, last)
                value = (
                    part[pl.ds(own + at, chunk), q * quarter : (q + 1) * quarter]
                    + recv_buf[0, up_k, pl.ds(at, chunk), :].astype(jnp.float32)
                    + recv_buf[1, down_k, pl.ds(at, chunk), :].astype(jnp.float32)
                )
                finish(at, chunk, q, value)
            return 0

        lax.fori_loop(0, 4, close, 0)
        return copies

    def keep_turned(at, chunk, q, value):
        turned[pl.ds(at, chunk), q * quarter : (q + 1) * quarter] = value.astype(jnp.bfloat16)

    def keep_rotated(at, chunk, q, value):
        rot_send[pl.ds(at, chunk), q * quarter : (q + 1) * quarter] = value

    copies_one = reduce(a_all, g_turned, s_one, v_one, 0, keep_turned)
    copies_two = reduce(l_all, turned, s_two, v_two, 1, keep_rotated)

    theirs_l = pl.ds(pl.multiple_of(other * rows, rows), rows)
    rot_copy = remote(rot_send.at[theirs_l, :], rot.at[c], pair_send.at[1], pair_recv.at[1], partner)
    rot_copy.start()
    rot[c] = rot_send[mine_l, :]
    rot_copy.wait_recv()
    for h in range(2):
        cols = slice(h * half, (h + 1) * half)
        turned_back = rot[h]
        first = BETA_ONE * m1[:, cols] + (1.0 - BETA_ONE) * turned_back
        second = BETA_TWO * m2[:, cols] + (1.0 - BETA_TWO) * turned_back * turned_back
        f_buf[:, cols] = first
        s_buf[:, cols] = second
        d_buf[:, cols] = (first / (jnp.sqrt(second) + EPS_DIVIDE)).astype(jnp.bfloat16)
    out_first = pltpu.make_async_copy(f_buf, first_out, out_sem.at[0])
    out_second = pltpu.make_async_copy(s_buf, second_out, out_sem.at[1])
    out_first.start()
    out_second.start()

    def restore(which):
        return lax.dot_general(
            d_buf[...], r_all[pl.ds(pl.multiple_of(which * half, half), half), :],
            (((1,), (1,)), ((), ())), preferred_element_type=jnp.float32,
        ).astype(jnp.bfloat16)

    def gather_rows(back, way, part_of):
        owner = mod(z - back, NZ) if way == 0 else mod(z + back, NZ)
        core = c if part_of ^ way == 0 else other
        return pl.ds(pl.multiple_of(owner * block + core * rows, rows), rows)

    res_send[...] = restore(other)
    res_copy = remote(res_send, x_all.at[gather_rows(0, 0, 0), :], pair_send.at[2], pair_recv.at[2], partner)
    res_copy.start()
    x_all[gather_rows(0, 0, 0), :] = restore(c)

    x_copies = []
    for k, (back, part_of) in enumerate(GATHER):
        ways = []
        for way, device in ((0, up), (1, down)):
            here = gather_rows(back, way, part_of)
            ways.append(remote(x_all.at[here, :], x_all.at[here, :], x_send.at[way, k], x_recv.at[way, k], device))
        x_copies.append(ways)

    def update_pair(i):
        which = lax.rem(z // 2 + i, NZ // 2)
        at = pl.multiple_of(which * pair_wide, pair_wide)
        return jnp.dot(l_all[:, pl.ds(at, pair_wide)], x_all[pl.ds(at, pair_wide), :], preferred_element_type=jnp.float32)

    x_copies[0][0].start()
    res_copy.wait_recv()
    x_copies[0][1].start()
    for way in range(2):
        x_copies[1][way].start()
    for k in range(2, len(GATHER)):
        for way in range(2):
            x_copies[k - 2][way].wait_recv()
            x_copies[k][way].start()
        if k == 3:
            upd[...] = update_pair(0)
    odd = lax.rem(z, 2)
    upd[...] += update_pair(3 - 2 * odd)
    for way in range(2):
        x_copies[5][way].wait_recv()
    upd[...] += update_pair(1 + 2 * odd)
    for way in range(2):
        x_copies[6][way].wait_recv()
    upd[...] += update_pair(2)

    squares = jnp.sum(upd[...] * upd[...])
    n_col[0] = jnp.broadcast_to(squares, n_col.shape[1:])
    upd_copy = remote(upd.at[theirs_l, :], upd_other, pair_send.at[3], pair_recv.at[3], partner)
    n_copies = [
        remote(n_col.at[0], n_col.at[1 + i], n_send.at[0, i], n_recv.at[0], device) for i, device in enumerate(column)
    ]
    for copy in n_copies:
        copy.start()
    upd_copy.start()
    remote(n_col.at[1:], n_col.at[1:], n_send.at[0, 0], n_recv.at[0], partner).wait_recv()
    total = jnp.zeros(n_col.shape[1:], jnp.float32)
    for d in range(NZ * NC):
        back_z = lax.rem(z - d // NC + NZ, NZ)
        back_c = lax.rem(c - d % NC + NC, NC)
        total = total + n_col[back_z * NC + back_c]
    n_exp[0] = total
    e_copies = [
        remote(n_exp.at[0], n_exp.at[1 + i], n_send.at[1, i], n_recv.at[1], device) for i, device in enumerate(plane)
    ]
    for copy in e_copies:
        copy.start()
    upd_copy.wait_recv()
    remote(n_exp.at[1:], n_exp.at[1:], n_send.at[1, 0], n_recv.at[1], partner).wait_recv()
    cells = float(width * hidden)
    own_norm = jnp.sqrt(total / cells + EPS_MEAN)
    norms = jnp.zeros_like(total)
    for e in range(NY * NX):
        norms = norms + jnp.sqrt(n_exp[e] / cells + EPS_MEAN)
    below = jnp.maximum(own_norm, norms / float(NY * NX))
    rms_out[...] = own_norm
    below = below[0:1, 0:1]
    own_half = upd[mine_l, :]
    other_half = upd_other[...]
    low = jnp.where(c == 0, own_half, other_half)
    high = jnp.where(c == 0, other_half, own_half)
    delta_out[:, :half] = (-low / below).astype(jnp.bfloat16)
    delta_out[:, half:] = (-high / below).astype(jnp.bfloat16)

    for copy in g_copies + a_copies + forwards + [l_copy, rot_copy, res_copy, upd_copy] + n_copies + e_copies:
        copy.wait_send()
    for ways in copies_one + copies_two + x_copies:
        for copy in ways:
            copy.wait_send()
    out_first.wait()
    out_second.wait()


def local(acts, grad_out, routing_counts, left_basis, right_basis, first_moment, second_moment):
    width, hidden = acts.shape[-1], grad_out.shape[-1]
    rows = left_basis.shape[1]
    block, half = 2 * rows, hidden // 2
    quarter = half // 2
    own_tokens = acts.shape[1] * acts.shape[2]
    both = 2 * own_tokens
    bf16, f32 = jnp.bfloat16, jnp.float32
    vmem, dma = pltpu.VMEM, pltpu.SemaphoreType.DMA
    hbm = pl.BlockSpec(memory_space=pl.ANY)
    whole = pl.BlockSpec(memory_space=pltpu.VMEM)
    messages = len(REDUCE)
    delta, first, second, rms = pl.pallas_call(
        kernel,
        name="soap_step",
        out_shape=(
            jax.ShapeDtypeStruct((rows, hidden), bf16),
            jax.ShapeDtypeStruct((rows, hidden), f32),
            jax.ShapeDtypeStruct((rows, hidden), f32),
            jax.ShapeDtypeStruct((8, 128), f32),
        ),
        in_specs=[pl.BlockSpec(memory_space=pltpu.SMEM)] + [hbm] * 6,
        out_specs=(whole, hbm, hbm, whole),
        scratch_shapes=[
            vmem((both, width), bf16),
            vmem((own_tokens, hidden), bf16),
            vmem((both, hidden), bf16),
            vmem((block, width), bf16),
            vmem((hidden, hidden), bf16),
            vmem((rows, hidden), f32),
            vmem((rows, hidden), f32),
            vmem((both, half), bf16),
            vmem((width, half), f32),
            vmem((2, messages, block, quarter), bf16),
            vmem((2, messages, block, quarter), bf16),
            vmem((2, messages, block, quarter), bf16),
            vmem((2, messages, block, quarter), bf16),
            vmem((block, half), bf16),
            vmem((2, rows, half), f32),
            vmem((block, half), f32),
            vmem((rows, half), bf16),
            vmem((width, half), bf16),
            vmem((block, half), f32),
            vmem((rows, half), f32),
            vmem((rows, hidden), bf16),
            vmem((rows, hidden), f32),
            vmem((rows, hidden), f32),
            vmem((NZ * NC, 8, 128), f32),
            vmem((NY * NX, 8, 128), f32),
            dma((6,)),
            dma((15,)), dma((15,)), dma((15,)), dma((15,)),
            dma((32,)), dma((2,)),
            dma((4,)), dma((4,)),
            dma((2, 2, messages)), dma((2, 2, messages)),
            dma((2, messages)), dma((2, messages)),
            dma((2, 15)), dma((2,)),
            dma((2,)),
        ],
        compiler_params=pltpu.CompilerParams(
            collective_id=0, has_side_effects=True, vmem_limit_bytes=64 * 1024 * 1024 - 128 * 1024
        ),
    )(
        routing_counts,
        acts.reshape(own_tokens, width),
        grad_out.reshape(own_tokens, hidden),
        left_basis[0],
        right_basis[0],
        first_moment[0],
        second_moment[0],
    )
    return delta[None], first[None], second[None], rms[0, :1]


def solution(mesh):
    split = Mesh(mesh.devices.reshape(NY, NX, NZ, NC), AXES)
    placed = (
        P(AXES, None, None, None),
        P(AXES, None, None, None),
        P(AXES, None),
        P(EXPERT, DP, None),
        P(EXPERT, None, None),
        P(EXPERT, DP, None),
        P(EXPERT, DP, None),
    )
    return jax.shard_map(
        local,
        mesh=split,
        in_specs=placed,
        out_specs=(P(EXPERT, DP, None), P(EXPERT, DP, None), P(EXPERT, DP, None), P(EXPERT)),
        check_vma=False,
    )
```

time: 319 us -> 179 us (0.56)
  waiting for transfers between devices: 176 us -> 0 us
  Pallas kernels: 0 us -> 172 us
  blocking collectives: 76.5 us -> 0 us
  matrix products: 21.8 us -> 0 us
  between operations: 15.1 us -> 0.65 us
  local copies, waits for them, and re-layouts: 20.3 us -> 6.21 us
  other arithmetic: 8.07 us -> 0 us
    pallas_call x0 -> x1, Pallas kernels: none -> 172 us  [local(): pl.pallas_call(kernel, name='soap_step', out_shape=(jax.ShapeDtypeStruct(...]
    reduce_scatter x1 -> x0, waiting for transfers between devices: 66.2 us -> none  [local(): lax.psum_scatter(jnp.einsum('tk,tf->kf', token_acts, token_grads, preferr...]
    unnamed x4 -> x0, waiting for transfers between devices: 63.7 us -> none
    all_gather x1 -> x0, waiting for transfers between devices: 46.2 us -> none  [local(): lax.all_gather(restored, DP, axis=0, tiled=True)]
    psum x4 -> x0, blocking collectives: 38.8 us -> none  [over_axes(): return functools.reduce(lax.psum, axes, x)]
    all_to_all x1 -> x0, blocking collectives: 37.8 us -> none  [sent_together(): lax.all_to_all(both, axis, split_axis=split_dim, concat_axis=concat_dim,...]
    dot_general x4 -> x0, matrix products: 21.8 us -> none  [the longest x1 7.2 us: local(): jnp.einsum('kc,kf->cf', basis_columns, right_turned, preferred_element_ty...]
    unnamed x12 -> x5, local copies, waits for them, and re-layouts: 20.3 us -> 4.94 us
  transfers between devices with their start and end apart: 3 -> 0, of which waited for: 3 -> 0; matrix products, arithmetic and copies ran while one was open for 3% -> 0% of each run, Pallas kernels for 0% -> 0%
where the time goes in v1:
time: 179 us; the launch traced here: 178 us
  Pallas kernels  172 us (96%)
  local copies, waits for them, and re-layouts  6.21 us (3%)
    pallas_call x1, Pallas kernels, local(): pl.pallas_call(kernel, name='soap_step', out_shape=(jax.ShapeDtypeStruct(...  172 us
    unnamed x5, local copies, waits for them, and re-layouts  4.94 us

profile of v1, /device:TPU:1, one launch (start us, length us, event | category | flops | bytes accessed | tf_op | source)
XLA Modules:
  0.0 178.4 jit_solution(2569542738753927625)
XLA Ops:
  0.6 171.5 %soap_step.1 = (bf16[224,1024]{1,0:T(8,128)(2,1)}, f32[224,1024]{1,0:T(8,128)}, f32[224,1024]{1,0:T(8,128)}, f32[8,128]{1,0:T(8,128)}) custom-call(s32[1,16]{1,0:T(1,128)} %counts.1, bf16[256,3584]{1,0:T(8,128)(2,1)} %bitcast.11, bf16[256,1024]{1,0:T(8,128)(2,1)} %bitcast.17, bf16[224,3584]{1,0:T(8,128)(2,1)} %bitcast.12, bf16[1024,1024]{1,0:T(8,128)(2,1)} %bitcast.10, ...), custom_call_target="tpu_custom_call" | custom-call | tf_op jit(solution)/shard_map/soap_step/pallas_call | solution.py:346
  172.2 0.0 copy-start
  172.2 1.3 slice.3
  173.5 1.8 %copy.14 = bf16[1,224,1024]{2,1,0:T(8,128)(2,1)} copy(bf16[1,224,1024]{2,1,0:T(8,128)(2,1)} %bitcast.18) | data formatting | bytes 917504
  175.3 2.2 %copy.15 = f32[1,224,1024]{2,1,0:T(8,128)} copy(f32[1,224,1024]{2,1,0:T(8,128)} %bitcast.14) | data formatting | bytes 1835008
  177.5 0.0 copy-done
  177.5 0.9 copy.16
Async XLA Ops:
  172.2 5.3 %copy-start = (f32[224,1024]{1,0:T(8,128)S(1)}, f32[224,1024]{1,0:T(8,128)}, u32[]{:S(2)}) copy-start(f32[224,1024]{1,0:T(8,128)} %get-tuple-element.10) | copy-start | bytes 2752516

commit v2 on v1

v2 whole, which is shorter than its diff:
```python
import functools

import jax
import jax.numpy as jnp
from jax import lax
from jax.experimental import pallas as pl
from jax.experimental.pallas import tpu as pltpu
from jax.sharding import Mesh
from jax.sharding import PartitionSpec as P

AXES = ("y", "x", "z", "core")
EXPERT = ("y", "x")
DP = ("z", "core")
NY, NX, NZ, NC = 4, 4, 8, 2
MESH = pl.DeviceIdType.MESH

BETA_ONE = 0.9
BETA_TWO = 0.95
EPS_DIVIDE = 1e-08
EPS_MEAN = 1e-06

PLANE = (
    (0, 1), (1, 0), (0, 3), (3, 0), (1, 1), (3, 3), (1, 3), (3, 1),
    (2, 0), (0, 2), (1, 2), (2, 1), (3, 2), (2, 3), (2, 2),
)
COLUMN = tuple((dz, dc) for dz in range(NZ) for dc in range(NC) if dz or dc)
ONE_UP = (
    (4, 0, 0), (4, 1, 1), (3, 1, 0), (3, 0, 1), (3, 0, 0), (3, 1, 1), (2, 1, 0),
    (2, 0, 0), (2, 0, 1), (1, 1, 0), (1, 0, 0), (2, 1, 1), (1, 0, 1), (1, 1, 1),
)
ONE = (ONE_UP, tuple((away, 1 - r, q) for away, r, q in ONE_UP))
TWO = (
    (
        (4, 0, 0), (3, 1, 0), (4, 1, 1), (3, 0, 1), (3, 0, 0), (2, 1, 0), (3, 1, 1),
        (2, 0, 1), (2, 0, 0), (1, 0, 1), (1, 0, 0), (2, 1, 1), (1, 1, 0), (1, 1, 1),
    ),
    (
        (4, 1, 0), (3, 0, 0), (4, 0, 1), (3, 1, 1), (3, 1, 0), (2, 0, 0), (3, 0, 1),
        (2, 1, 1), (2, 0, 1), (1, 0, 0), (1, 0, 1), (2, 1, 0), (1, 1, 1), (1, 1, 0),
    ),
)
NEAR = tuple((back, r, q) for back in range(3) for r in range(2) for q in range(2))
GATHER = (NEAR + ((3, 0, 0), (3, 0, 1)), NEAR + ((3, 1, 0), (3, 1, 1)))
MESSAGES = len(ONE_UP)


def before(table, message):
    away, r, q = message
    return {m: k for k, m in enumerate(table)}.get((away + 1, r, q))


def kernel(
    counts_in, acts, grads, left, right, first_in, second_in,
    delta_out, first_out, second_out, rms_out,
    counts, a_all, g_own, g_all, l_all, l_turn, r_all, m1, m2, g_turned, part, s_one, v_one, s_two, v_two,
    turned, rot_own, rot_in, res_send, x_all, upd, upd_other, d_buf, f_buf, s_buf, n_col, n_exp,
    load_sem, t_send, t_recv, fwd_send, fwd_recv, pair_send, pair_recv,
    r_send, r_recv, x_send, x_recv, n_send, n_recv, out_sem,
):
    y, x, z, c = (lax.axis_index(a) for a in AXES)
    other = 1 - c
    rows = left.shape[0]
    block = 2 * rows
    width = left.shape[1]
    hidden = grads.shape[1]
    half = hidden // 2
    quarter = half // 2
    slots = acts.shape[0] // (NY * NX)
    tokens = NY * NX * slots
    pair_wide = 2 * block

    def mod(v, n):
        return lax.rem(v + n, n)

    partner = (y, x, z, other)
    plane = [(mod(y + dy, NY), mod(x + dx, NX), z, c) for dy, dx in PLANE]
    column = [(y, x, mod(z + dz, NZ), mod(c + dc, NC)) for dz, dc in COLUMN]
    up = (y, x, mod(z + 1, NZ), c)
    down = (y, x, mod(z - 1, NZ), c)

    def remote(src, dst, send, recv, device):
        return pltpu.make_async_remote_copy(
            src_ref=src, dst_ref=dst, send_sem=send, recv_sem=recv, device_id=device, device_id_type=MESH
        )

    barrier = pltpu.get_barrier_semaphore()
    for device in plane + column:
        pl.semaphore_signal(barrier, 1, device_id=device, device_id_type=MESH)

    own_expert = y * NX + x
    mine_l = pl.ds(pl.multiple_of(c * rows, rows), rows)
    load_c = pltpu.make_async_copy(counts_in, counts, load_sem.at[6])
    load_g = pltpu.make_async_copy(grads, g_own, load_sem.at[0])
    load_a = pltpu.make_async_copy(
        acts.at[pl.ds(pl.multiple_of(own_expert * slots, slots), slots), :],
        a_all.at[pl.ds(pl.multiple_of(c * tokens, tokens), slots), :],
        load_sem.at[1],
    )
    load_l = pltpu.make_async_copy(left, l_all.at[mine_l, :], load_sem.at[2])
    load_r = pltpu.make_async_copy(right, r_all, load_sem.at[3])
    load_m1 = pltpu.make_async_copy(first_in, m1, load_sem.at[4])
    load_m2 = pltpu.make_async_copy(second_in, m2, load_sem.at[5])
    load_c.start()
    load_g.start()
    load_l.start()
    load_c.wait()
    load_g.wait()
    for load in (load_a, load_r, load_m1, load_m2):
        load.start()
    slot_index = lax.broadcasted_iota(jnp.int32, (slots, hidden), 0)
    for e in range(NY * NX):
        here = slice(e * slots, (e + 1) * slots)
        g_own[here, :] = jnp.where(slot_index < counts[0, e], g_own[here, :].astype(jnp.float32), 0.0).astype(jnp.bfloat16)
    pl.semaphore_wait(barrier, len(plane) + len(column))

    odd = lax.rem(z, 2)
    pair_of = [
        lax.rem(z // 2 + i, NZ // 2) * pair_wide for i in (2, 1 + 2 * odd, 3 - 2 * odd, 0)
    ]
    pairs = [pl.ds(pl.multiple_of(at, pair_wide), pair_wide) for at in pair_of]
    wide, rest = pair_wide * 4 // 7, pair_wide * 3 // 7

    def window(at, size):
        return pl.ds(pl.multiple_of(at, pair_wide // 7), size)

    groups = [None]
    for one, two in ((0, 1), (2, 3)):
        groups += [
            window(pair_of[one] + rest * odd, wide),
            window(pair_of[two] + rest * (1 - odd), wide),
            window(pair_of[one] + wide * (1 - odd), rest),
            window(pair_of[two] + wide * odd, rest),
        ]

    def token_rows(core, i):
        return pl.ds(pl.multiple_of(core * tokens + i * slots, slots), slots)

    t_copies = []
    for g, cols in enumerate(groups):
        copies = []
        for i, device in enumerate(plane):
            expert = device[0] * NX + device[1]
            src = pl.ds(pl.multiple_of(expert * slots, slots), slots)
            dst = token_rows(c, i + 1)
            if g == 0:
                ends = g_own.at[src, :], g_all.at[dst, :]
            else:
                ends = acts.at[src, cols], a_all.at[dst, cols]
            copies.append(remote(*ends, t_send.at[g], t_recv.at[g], device))
        t_copies.append(copies)

    def token_start(g):
        for copy in t_copies[g]:
            copy.start()

    def group_of(g, core, first, count):
        here = pl.ds(pl.multiple_of(core * tokens + first, slots), count)
        return g_all.at[here, :] if g == 0 else a_all.at[here, groups[g]]

    def token_wait(g):
        arrived = group_of(g, c, slots, tokens - slots)
        return remote(arrived, arrived, t_send.at[g], t_recv.at[g], partner)

    forwards = []
    for g in range(len(groups)):
        mine = group_of(g, c, 0, tokens)
        forwards.append(remote(mine, mine, fwd_send.at[g], fwd_recv.at[g], partner))

    def token_finish(g):
        token_wait(g).wait_recv()
        forwards[g].start()
        if g + 3 < len(groups):
            token_wait(g).wait_send()
            token_start(g + 3)
        theirs = group_of(g, other, 0, tokens)
        remote(theirs, theirs, fwd_send.at[g], fwd_recv.at[g], partner).wait_recv()

    for g in range(3):
        token_start(g)
    own_g = pl.ds(pl.multiple_of(own_expert * slots, slots), slots)
    g_all[token_rows(c, 0), :] = g_own[own_g, :]
    load_l.wait()
    l_copy = remote(l_all.at[mine_l, :], l_all.at[mine_l, :], pair_send.at[0], pair_recv.at[0], partner)
    l_copy.start()
    load_a.wait()
    load_r.wait()
    load_m1.wait()
    load_m2.wait()
    l_copy.wait_recv()
    for p in range(NZ // 2):
        at = slice(p * pair_wide, (p + 1) * pair_wide)
        l_turn[at, :] = l_all[:, at].T
    token_finish(0)
    g_turned[...] = jnp.dot(
        g_all[...], r_all[:, pl.ds(pl.multiple_of(c * half, half), half)], preferred_element_type=jnp.float32
    ).astype(jnp.bfloat16)

    chunk = rows // 2

    def message(tables, send_buf, recv_buf, sems, k, way):
        return remote(
            send_buf.at[way, k], recv_buf.at[way, k], r_send.at[sems, way, k], r_recv.at[sems, way, k], (up, down)[way]
        )

    def send(tables, send_buf, recv_buf, sems, k):
        for way in range(2):
            away, r, q = tables[way][k]
            owner = mod(z + away, NZ) if way == 0 else mod(z - away, NZ)
            start = owner * block + r * rows
            added = before(tables[way], tables[way][k])
            if added is not None:
                message(tables, send_buf, recv_buf, sems, added, way).wait_recv()

            def one(t, _):
                at = pl.multiple_of(t * chunk, chunk)
                value = part[pl.ds(pl.multiple_of(start + at, chunk), chunk), q * quarter : (q + 1) * quarter]
                if added is not None:
                    value = value + recv_buf[way, added, pl.ds(at, chunk), :].astype(jnp.float32)
                send_buf[way, k, pl.ds(at, chunk), :] = value.astype(jnp.bfloat16)
                return 0

            lax.fori_loop(0, 2, one, 0)
            message(tables, send_buf, recv_buf, sems, k, way).start()

    def close(tables, send_buf, recv_buf, sems, r, q, store):
        k = [tables[way].index((1, r, q)) for way in range(2)]
        for way in range(2):
            message(tables, send_buf, recv_buf, sems, k[way], way).wait_recv()
        start = z * block + r * rows

        def one(t, _):
            at = pl.multiple_of(t * chunk, chunk)
            value = part[pl.ds(pl.multiple_of(start + at, chunk), chunk), q * quarter : (q + 1) * quarter]
            for way in range(2):
                value = value + recv_buf[way, k[way], pl.ds(at, chunk), :].astype(jnp.float32)
            store(r, q, pl.ds(at, chunk), value)
            return 0

        lax.fori_loop(0, 2, one, 0)

    first_sum = (ONE, s_one, v_one, 0)
    second_sum = (TWO, s_two, v_two, 1)

    def gradient_part(g):
        token_finish(g)
        part[groups[g], :] = lax.dot_general(
            a_all[:, groups[g]], g_turned[...], (((0,), (0,)), ((), ())), preferred_element_type=jnp.float32
        )

    def keep_turned(r, q, at, value):
        turned[r, at, q * quarter : (q + 1) * quarter] = value.astype(jnp.bfloat16)

    def rotated_part(p, q):
        cols = slice(q * quarter, (q + 1) * quarter)
        part[pairs[p], cols] = jnp.dot(
            l_turn[pairs[p], :], turned[...].reshape(block, half)[:, cols], preferred_element_type=jnp.float32
        )

    def keep_rotated(r, q, at, value):
        rot_own[r, at, q * quarter : (q + 1) * quarter] = value

    for g, ready in ((1, (0, 1)), (2, ()), (3, (2, 3, 4, 5)), (4, ()), (5, (6, 7, 8)), (6, ()), (7, (9, 10)), (8, (11, 12))):
        gradient_part(g)
        for k in ready:
            send(*first_sum, k)
    for r in range(2):
        close(*first_sum, r, 0, keep_turned)
    send(*first_sum, 13)
    rotated_part(0, 0)
    send(*second_sum, 0)
    rotated_part(1, 0)
    send(*second_sum, 1)
    rotated_part(2, 0)
    rotated_part(3, 0)
    for r in range(2):
        close(*first_sum, r, 1, keep_turned)
    rotated_part(0, 1)
    send(*second_sum, 2)
    rotated_part(1, 1)
    send(*second_sum, 3)
    rotated_part(2, 1)
    rotated_part(3, 1)
    for k in range(4, 13):
        send(*second_sum, k)

    rot_copy = remote(rot_own.at[other], rot_in, pair_send.at[1], pair_recv.at[1], partner)
    x_rows = [pl.ds(pl.multiple_of(z * block + r * rows, rows), rows) for r in range(2)]
    res_copies = [remote(res_send, x_all.at[x_rows[r], :], pair_send.at[2], pair_recv.at[2], partner) for r in range(2)]
    out_first = pltpu.make_async_copy(f_buf, first_out, out_sem.at[0])
    out_second = pltpu.make_async_copy(s_buf, second_out, out_sem.at[1])

    def gather_message(k, way):
        back, r, q = GATHER[way][k]
        owner = mod(z - back, NZ) if way == 0 else mod(z + back, NZ)
        here = x_all.at[
            pl.ds(pl.multiple_of(owner * block + r * rows, rows), rows), q * quarter : (q + 1) * quarter
        ]
        return remote(here, here, x_send.at[way, k], x_recv.at[way, k], (up, down)[way])

    def close_rotated(r):
        for q in range(2):
            close(*second_sum, r, q, keep_rotated)

        @pl.when(c != r)
        def _():
            rot_copy.start()

    def restore(r):
        @pl.when(c == r)
        def _():
            rot_copy.wait_recv()
            for h in range(2):
                cols = slice(h * half, (h + 1) * half)
                turned_back = rot_own[r] if h == r else rot_in[...]
                first = BETA_ONE * m1[:, cols] + (1.0 - BETA_ONE) * turned_back
                second = BETA_TWO * m2[:, cols] + (1.0 - BETA_TWO) * turned_back * turned_back
                f_buf[:, cols] = first
                s_buf[:, cols] = second
                d_buf[:, cols] = (first / (jnp.sqrt(second) + EPS_DIVIDE)).astype(jnp.bfloat16)

            def half_of(which):
                return lax.dot_general(
                    d_buf[...], r_all[which * half : (which + 1) * half, :],
                    (((1,), (1,)), ((), ())), preferred_element_type=jnp.float32,
                ).astype(jnp.bfloat16)

            res_send[...] = half_of(1 - r)
            res_copies[r].start()
            x_all[x_rows[r], :] = half_of(r)

        @pl.when(c != r)
        def _():
            res_copies[r].wait_recv()

        for k in (2 * r, 2 * r + 1):
            for way in range(2):
                gather_message(k, way).start()

    close_rotated(0)
    send(*second_sum, 13)
    restore(0)
    close_rotated(1)
    restore(1)
    out_first.start()
    out_second.start()

    def add_update(at, first=False):
        value = jnp.dot(l_all[:, at], x_all[at, :], preferred_element_type=jnp.float32)
        upd[...] = value if first else upd[...] + value

    def arrived(way, k):
        gather_message(k, way).wait_recv()

    for k in range(4, MESSAGES):
        for way in range(2):
            arrived(way, before(tuple((-b, r, q) for b, r, q in GATHER[way]), (-GATHER[way][k][0], *GATHER[way][k][1:])))
            gather_message(k, way).start()
        if k == 7:
            add_update(pairs[3], first=True)
        if k == 11:
            add_update(pairs[2])
    for way, rest_of in ((0, (10, 11)), (1, (8, 9))):
        for k in rest_of:
            arrived(way, k)
    add_update(pairs[1])
    add_update(groups[3])
    for way in range(2):
        for k in (12, 13):
            arrived(way, k)
    add_update(groups[1])

    squares = jnp.sum(upd[...] * upd[...])
    n_col[0] = jnp.broadcast_to(squares, n_col.shape[1:])
    theirs_l = pl.ds(pl.multiple_of(other * rows, rows), rows)
    upd_copy = remote(upd.at[theirs_l, :], upd_other, pair_send.at[3], pair_recv.at[3], partner)
    n_copies = [
        remote(n_col.at[0], n_col.at[1 + i], n_send.at[0, i], n_recv.at[0], device) for i, device in enumerate(column)
    ]
    for copy in n_copies:
        copy.start()
    upd_copy.start()
    remote(n_col.at[1:], n_col.at[1:], n_send.at[0, 0], n_recv.at[0], partner).wait_recv()
    total = jnp.zeros(n_col.shape[1:], jnp.float32)
    for d in range(NZ * NC):
        back_z = lax.rem(z - d // NC + NZ, NZ)
        back_c = lax.rem(c - d % NC + NC, NC)
        total = total + n_col[back_z * NC + back_c]
    n_exp[0] = total
    e_copies = [
        remote(n_exp.at[0], n_exp.at[1 + i], n_send.at[1, i], n_recv.at[1], device) for i, device in enumerate(plane)
    ]
    for copy in e_copies:
        copy.start()
    upd_copy.wait_recv()
    remote(n_exp.at[1:], n_exp.at[1:], n_send.at[1, 0], n_recv.at[1], partner).wait_recv()
    cells = float(width * hidden)
    own_norm = jnp.sqrt(total / cells + EPS_MEAN)
    norms = jnp.zeros_like(total)
    for e in range(NY * NX):
        norms = norms + jnp.sqrt(n_exp[e] / cells + EPS_MEAN)
    below = jnp.maximum(own_norm, norms / float(NY * NX))
    rms_out[0] = jnp.max(own_norm)
    below = below[0:1, 0:1]
    own_half = upd[mine_l, :]
    other_half = upd_other[...]
    low = jnp.where(c == 0, own_half, other_half)
    high = jnp.where(c == 0, other_half, own_half)
    delta_out[:, :half] = (-low / below).astype(jnp.bfloat16)
    delta_out[:, half:] = (-high / below).astype(jnp.bfloat16)

    for g in range(len(groups) - 3, len(groups)):
        token_wait(g).wait_send()
    for copy in forwards + [l_copy, rot_copy, res_copies[0], upd_copy] + n_copies + e_copies:
        copy.wait_send()
    for k in range(MESSAGES):
        for way in range(2):
            message(*first_sum, k, way).wait_send()
            message(*second_sum, k, way).wait_send()
            gather_message(k, way).wait_send()
    out_first.wait()
    out_second.wait()


def local(acts, grad_out, routing_counts, left_basis, right_basis, first_moment, second_moment):
    width, hidden = acts.shape[-1], grad_out.shape[-1]
    rows = left_basis.shape[1]
    block, half = 2 * rows, hidden // 2
    quarter = half // 2
    own_tokens = acts.shape[1] * acts.shape[2]
    both = 2 * own_tokens
    bf16, f32 = jnp.bfloat16, jnp.float32
    vmem, dma = pltpu.VMEM, pltpu.SemaphoreType.DMA
    hbm = pl.BlockSpec(memory_space=pltpu.HBM)
    anywhere = pl.BlockSpec(memory_space=pl.ANY)
    scalars = pl.BlockSpec(memory_space=pltpu.SMEM)
    whole = pl.BlockSpec(memory_space=pltpu.VMEM)
    delta, first, second, rms = pl.pallas_call(
        kernel,
        name="soap_step",
        out_shape=(
            jax.ShapeDtypeStruct((rows, hidden), bf16),
            jax.ShapeDtypeStruct((rows, hidden), f32),
            jax.ShapeDtypeStruct((rows, hidden), f32),
            jax.ShapeDtypeStruct((1,), f32),
        ),
        in_specs=[hbm] * 7,
        out_specs=(whole, anywhere, anywhere, scalars),
        scratch_shapes=[
            pltpu.SMEM((1, NY * NX), jnp.int32),
            vmem((both, width), bf16),
            vmem((own_tokens, hidden), bf16),
            vmem((both, hidden), bf16),
            vmem((block, width), bf16),
            vmem((width, block), bf16),
            vmem((hidden, hidden), bf16),
            vmem((rows, hidden), f32),
            vmem((rows, hidden), f32),
            vmem((both, half), bf16),
            vmem((width, half), f32),
            vmem((2, MESSAGES, rows, quarter), bf16),
            vmem((2, MESSAGES, rows, quarter), bf16),
            vmem((2, MESSAGES, rows, quarter), bf16),
            vmem((2, MESSAGES, rows, quarter), bf16),
            vmem((2, rows, half), bf16),
            vmem((2, rows, half), f32),
            vmem((rows, half), f32),
            vmem((rows, half), bf16),
            vmem((width, half), bf16),
            vmem((block, half), f32),
            vmem((rows, half), f32),
            vmem((rows, hidden), bf16),
            vmem((rows, hidden), f32),
            vmem((rows, hidden), f32),
            vmem((NZ * NC, 8, 128), f32),
            vmem((NY * NX, 8, 128), f32),
            dma((7,)),
            dma((9,)), dma((9,)), dma((9,)), dma((9,)),
            dma((4,)), dma((4,)),
            dma((2, 2, MESSAGES)), dma((2, 2, MESSAGES)),
            dma((2, MESSAGES)), dma((2, MESSAGES)),
            dma((2, 15)), dma((2,)),
            dma((2,)),
        ],
        compiler_params=pltpu.CompilerParams(
            collective_id=0, has_side_effects=True, vmem_limit_bytes=52 * 1024 * 1024
        ),
    )(
        routing_counts,
        acts.reshape(own_tokens, width),
        grad_out.reshape(own_tokens, hidden),
        left_basis[0],
        right_basis[0],
        first_moment[0],
        second_moment[0],
    )
    return delta[None], first[None], second[None], rms


def solution(mesh):
    split = Mesh(mesh.devices.reshape(NY, NX, NZ, NC), AXES)
    placed = (
        P(AXES, None, None, None),
        P(AXES, None, None, None),
        P(AXES, None),
        P(EXPERT, DP, None),
        P(EXPERT, None, None),
        P(EXPERT, DP, None),
        P(EXPERT, DP, None),
    )
    return jax.shard_map(
        local,
        mesh=split,
        in_specs=placed,
        out_specs=(P(EXPERT, DP, None), P(EXPERT, DP, None), P(EXPERT, DP, None), P(EXPERT)),
        check_vma=False,
    )
```

time: 179 us -> 153 us (0.85)
  Pallas kernels: 172 us -> 146 us
  local copies, waits for them, and re-layouts: 6.21 us -> 4.31 us
  between operations: 0.65 us -> 2.46 us
    pallas_call x1, Pallas kernels: 172 us -> 146 us  [local(): pl.pallas_call(kernel, name='soap_step', out_shape=(jax.ShapeDtypeStruct(...]
    unnamed x5 -> x9, local copies, waits for them, and re-layouts: 4.94 us -> 4.31 us
where the time goes in v2:
time: 153 us
  Pallas kernels  146 us (95%)
  local copies, waits for them, and re-layouts  4.31 us (3%)
  between operations  2.46 us (2%)
    pallas_call x1, Pallas kernels, local(): pl.pallas_call(kernel, name='soap_step', out_shape=(jax.ShapeDtypeStruct(...  146 us
    unnamed x9, local copies, waits for them, and re-layouts  4.31 us

profile of v2, /device:TPU:1, one launch (start us, length us, event | category | flops | bytes accessed | tf_op | source)
XLA Modules:
  0.0 152.6 jit_solution(3484469517516931574)
XLA Ops:
  0.6 0.0 copy-start
  0.6 1.0 copy-done
  1.7 0.0 copy-start.1
  1.7 0.7 copy-done.1
  2.3 145.9 %soap_step.1 = (bf16[224,1024]{1,0:T(8,128)(2,1)S(1)}, f32[224,1024]{1,0:T(8,128)S(1)}, f32[224,1024]{1,0:T(8,128)}, f32[1]{0:T(128)}) custom-call(s32[1,16]{1,0:T(1,128)S(1)} %copy-done.1, bf16[256,3584]{1,0:T(8,128)(2,1)} %bitcast.13, bf16[256,1024]{1,0:T(8,128)(2,1)S(1)} %bitcast.10, bf16[224,3584]{1,0:T(8,128)(2,1)} %bitcast.14, ...), custom_call_target="tpu_custom_call" | custom-call | tf_op jit(solution)/shard_map/soap_step/pallas_call | solution.py:437
  148.2 0.0 copy-start.2
  148.2 0.8 copy.15
  149.0 0.9 copy.16
  149.9 0.0 copy-done.2
  149.9 0.9 copy.17
Async XLA Ops:
  0.6 1.0 copy-start
  1.7 0.7 copy-start.1
  148.2 1.7 %copy-start.2 = (f32[224,1024]{1,0:T(8,128)S(1)}, f32[224,1024]{1,0:T(8,128)}, u32[]{:S(2)}) copy-start(f32[224,1024]{1,0:T(8,128)} %get-tuple-element.10) | copy-start | bytes 2752516

commit v3 on v2

--- a/solution.py
+++ b/solution.py
@@ -20,8 +20,8 @@
 EPS_MEAN = 1e-06
 
 PLANE = (
-    (0, 1), (1, 0), (0, 3), (3, 0), (1, 1), (3, 3), (1, 3), (3, 1),
-    (2, 0), (0, 2), (1, 2), (2, 1), (3, 2), (2, 3), (2, 2),
+    (0, 1), (3, 0), (2, 2), (0, 3), (1, 0), (1, 2), (3, 2), (1, 1),
+    (3, 3), (2, 1), (2, 3), (1, 3), (3, 1), (0, 2), (2, 0),
 )
 COLUMN = tuple((dz, dc) for dz in range(NZ) for dc in range(NC) if dz or dc)
 ONE_UP = (
@@ -371,14 +371,25 @@
 
     squares = jnp.sum(upd[...] * upd[...])
     n_col[0] = jnp.broadcast_to(squares, n_col.shape[1:])
-    theirs_l = pl.ds(pl.multiple_of(other * rows, rows), rows)
-    upd_copy = remote(upd.at[theirs_l, :], upd_other, pair_send.at[3], pair_recv.at[3], partner)
     n_copies = [
         remote(n_col.at[0], n_col.at[1 + i], n_send.at[0, i], n_recv.at[0], device) for i, device in enumerate(column)
     ]
     for copy in n_copies:
         copy.start()
+    theirs_l = pl.ds(pl.multiple_of(other * rows, rows), rows)
+    upd_copy = remote(upd.at[theirs_l, :], upd_other, pair_send.at[3], pair_recv.at[3], partner)
     upd_copy.start()
+    for g in range(len(groups) - 3, len(groups)):
+        token_wait(g).wait_send()
+    for copy in forwards + [l_copy, rot_copy, res_copies[0]]:
+        copy.wait_send()
+    for k in range(MESSAGES):
+        for way in range(2):
+            message(*first_sum, k, way).wait_send()
+            message(*second_sum, k, way).wait_send()
+            gather_message(k, way).wait_send()
+    out_first.wait()
+    out_second.wait()
     remote(n_col.at[1:], n_col.at[1:], n_send.at[0, 0], n_recv.at[0], partner).wait_recv()
     total = jnp.zeros(n_col.shape[1:], jnp.float32)
     for d in range(NZ * NC):
@@ -391,34 +402,39 @@
     ]
     for copy in e_copies:
         copy.start()
-    upd_copy.wait_recv()
-    remote(n_exp.at[1:], n_exp.at[1:], n_send.at[1, 0], n_recv.at[1], partner).wait_recv()
     cells = float(width * hidden)
     own_norm = jnp.sqrt(total / cells + EPS_MEAN)
+    rms_out[0] = jnp.max(own_norm)
+    upd_copy.wait_recv()
+    own_half = upd[mine_l, :]
+    other_half = upd_other[...]
+    f_buf[:, :half] = jnp.where(c == 0, own_half, other_half)
+    f_buf[:, half:] = jnp.where(c == 0, other_half, own_half)
+    upd_copy.wait_send()
+    for copy in n_copies:
+        copy.wait_send()
+    remote(n_exp.at[1:], n_exp.at[1:], n_send.at[1, 0], n_recv.at[1], partner).wait_recv()
     norms = jnp.zeros_like(total)
     for e in range(NY * NX):
         norms = norms + jnp.sqrt(n_exp[e] / cells + EPS_MEAN)
-    below = jnp.maximum(own_norm, norms / float(NY * NX))
-    rms_out[0] = jnp.max(own_norm)
-    below = below[0:1, 0:1]
-    own_half = upd[mine_l, :]
-    other_half = upd_other[...]
-    low = jnp.where(c == 0, own_half, other_half)
-    high = jnp.where(c == 0, other_half, own_half)
-    delta_out[:, :half] = (-low / below).astype(jnp.bfloat16)
-    delta_out[:, half:] = (-high / below).astype(jnp.bfloat16)
-
-    for g in range(len(groups) - 3, len(groups)):
-        token_wait(g).wait_send()
-    for copy in forwards + [l_copy, rot_copy, res_copies[0], upd_copy] + n_copies + e_copies:
+    scale = -1.0 / jnp.maximum(own_norm, norms / float(NY * NX))
+    delta_out[...] = (f_buf[...] * scale[0:1, 0:1]).astype(jnp.bfloat16)
+    for copy in e_copies:
         copy.wait_send()
-    for k in range(MESSAGES):
-        for way in range(2):
-            message(*first_sum, k, way).wait_send()
-            message(*second_sum, k, way).wait_send()
-            gather_message(k, way).wait_send()
-    out_first.wait()
-    out_second.wait()
+
+
+def hand_on(*refs):
+    count = (len(refs) - 1) // 3
+    sources, results, held, sem = refs[:count], refs[count : 2 * count], refs[2 * count : 3 * count], refs[-1]
+    loads = [pltpu.make_async_copy(a, v, sem.at[0, i]) for i, (a, v) in enumerate(zip(sources, held))]
+    stores = [pltpu.make_async_copy(v, o, sem.at[1, i]) for i, (v, o) in enumerate(zip(held, results))]
+    for load in loads:
+        load.start()
+    for load, store in zip(loads, stores):
+        load.wait()
+        store.start()
+    for store in stores:
+        store.wait()
 
 
 def local(acts, grad_out, routing_counts, left_basis, right_basis, first_moment, second_moment):
@@ -471,8 +487,8 @@
             vmem((rows, hidden), bf16),
             vmem((rows, hidden), f32),
             vmem((rows, hidden), f32),
-            vmem((NZ * NC, 8, 128), f32),
-            vmem((NY * NX, 8, 128), f32),
+            vmem((NZ * NC, 1, 128), f32),
+            vmem((NY * NX, 1, 128), f32),
             dma((7,)),
             dma((9,)), dma((9,)), dma((9,)), dma((9,)),
             dma((4,)), dma((4,)),
@@ -482,7 +498,7 @@
             dma((2,)),
         ],
         compiler_params=pltpu.CompilerParams(
-            collective_id=0, has_side_effects=True, vmem_limit_bytes=52 * 1024 * 1024
+            collective_id=0, has_side_effects=True, vmem_limit_bytes=58000 * 1024
         ),
     )(
         routing_counts,
@@ -493,6 +509,15 @@
         first_moment[0],
         second_moment[0],
     )
+    results = (second, first, delta)
+    second, first, delta = pl.pallas_call(
+        hand_on,
+        name="hand_on",
+        out_shape=tuple(jax.ShapeDtypeStruct(a.shape, a.dtype) for a in results),
+        in_specs=[anywhere] * 3,
+        out_specs=(anywhere,) * 3,
+        scratch_shapes=[vmem(a.shape, a.dtype) for a in results] + [dma((2, 3))],
+    )(*results)
     return delta[None], first[None], second[None], rms
 
 

time: 153 us -> 149 us (0.974)
  local copies, waits for them, and re-layouts: 4.31 us -> 0 us
    unnamed x9 -> x0, local copies, waits for them, and re-layouts: 4.31 us -> none
    pallas_call x0 -> x1, Pallas kernels: none -> 2.6 us  [local(): pl.pallas_call(hand_on, name='hand_on', out_shape=tuple((jax.ShapeDtypeSt...]
    pallas_call x1, Pallas kernels: 146 us -> 144 us  [local(): pl.pallas_call(kernel, name='soap_step', out_shape=(jax.ShapeDtypeStruct(...]
where the time goes in v3:
time: 149 us
  Pallas kernels  146 us (98%)
  between operations  2.41 us (2%)
    pallas_call x1, Pallas kernels, local(): pl.pallas_call(kernel, name='soap_step', out_shape=(jax.ShapeDtypeStruct(...  144 us

profile of v3, /device:TPU:1, one launch (start us, length us, event | category | flops | bytes accessed | tf_op | source)
XLA Modules:
  0.0 148.7 jit_solution(11395709304407451265)
XLA Ops:
  0.6 143.7 %soap_step.1 = (bf16[224,1024]{1,0:T(8,128)(2,1)}, f32[224,1024]{1,0:T(8,128)}, f32[224,1024]{1,0:T(8,128)}, f32[1]{0:T(128)}) custom-call(s32[1,16]{1,0:T(1,128)} %counts_in.1, bf16[256,3584]{1,0:T(8,128)(2,1)} %bitcast.10, bf16[256,1024]{1,0:T(8,128)(2,1)} %bitcast.14, bf16[224,3584]{1,0:T(8,128)(2,1)} %bitcast.11, bf16[1024,1024]{1,0:T(8,128)(2,1)} %bitcast.9, ...), custom_call_target="tpu_custom_call" | custom-call | tf_op jit(solution)/shard_map/soap_step/pallas_call | solution.py:453
  144.4 2.6 %hand_on.1 = (f32[224,1024]{1,0:T(8,128)}, f32[224,1024]{1,0:T(8,128)}, bf16[224,1024]{1,0:T(8,128)(2,1)}) custom-call(f32[224,1024]{1,0:T(8,128)} %get-tuple-element.11.refs_0_, f32[224,1024]{1,0:T(8,128)} %get-tuple-element.12.refs_1_, bf16[224,1024]{1,0:T(8,128)(2,1)} %get-tuple-element.13.refs_2_), custom_call_target="tpu_custom_call" | custom-call | tf_op jit(solution)/shard_map/hand_on/pallas_call | solution.py:513
